TPU v7x, 256 devices: a whole 4x4x8 slice. The times are simulated.
256 devices in a mesh: band: 128 (over z, y, x), ch: 2 (over core).
Axes of the slice: x: 4, y: 4, z: 8, core: 2. Of those that a mesh axis runs over, the one named last changes fastest.
Arguments:
- grid_field: bfloat16 [100, 2097152], P(None, 'band'), may hold values from -6 to 6
- band_points: int32 [128], P('band'), may hold values from 8192 to 16384
- block_ids: int32 [128, 16], P('band'), may hold values from 0 to 4095, as said below
- block_count: int32 [128], P('band'), may hold values from 8 to 16
- block_weight: bfloat16 [128, 16, 256, 512], P('band'), may hold values from 0 to 0.039794922
- embed_weight: bfloat16 [100, 1024], P(None, 'ch'), may hold values from -0.3125 to 0.3125
- edge_src: int32 [655360], P('band'), may hold values from 0 to 32767, as said below
- edge_dst: int32 [655360], P('band'), may hold values from 0 to 32767, as said below
- edge_in_weight: bfloat16 [2, 1024, 1024], P(None, None, 'ch'), may hold values from -0.1875 to 0.1875
- edge_out_weight: bfloat16 [1024, 1024], P('ch'), may hold values from -0.0625 to 0.0625
- node_in_weight: bfloat16 [2, 1024, 1024], P(None, None, 'ch'), may hold values from -0.125 to 0.125
- node_out_weight: bfloat16 [1024, 1024], P('ch'), may hold values from -0.1875 to 0.1875
Outputs:
- node_state: bfloat16 [32768, 1024], P('band', 'ch')
Inputs may be any that keep to these rules, and one draw needn't show every extreme that they name: For band b, block_ids[b, k] * 512 lies from max(b * 16384 - 16384 // 2, 0) to min((b + 1) * 16384 + 16384 // 2, 2097152) - 512; both ends are named by every band; ids may repeat. `edge_src`: edge e belongs to band b = e // 5120; its source node lies in bands b - 1 to b + 1 of the mesh. `edge_dst`: edge e ends at a node of its band b = e // 5120.
All inputs are finite; a program needn't handle non-finite values.
Results may differ from a plain program's by a relative error of at most 0.015.
Values may be sent and summed in bfloat16 or wider, within the bound.
No kernel may reach another device: no remote copies, remote signals or barrier semaphores. Data moves between devices by JAX's collectives and lax.ppermute only.
A program may use at most 64 MiB of HBM per device.

v0:
```python
import jax
import jax.numpy as jnp
from jax import lax
from jax.sharding import PartitionSpec as P


def extended_2(block, sides, width):
    for axis, dim in sides:
        count = lax.axis_size(axis)
        forward = [(i, i + 1) for i in range(count - 1)]
        backward = [(target, source) for source, target in forward]
        low = lax.ppermute(
            lax.slice_in_dim(block, block.shape[dim] - width, None, axis=dim), axis, forward
        )
        high = lax.ppermute(lax.slice_in_dim(block, 0, width, axis=dim), axis, backward)
        block = jnp.concatenate([low, block, high], axis=dim)
    return block


def sent_to_all(x, axis):
    copies = jnp.broadcast_to(x, (lax.axis_size(axis), *x.shape))
    return lax.all_to_all(copies, axis, split_axis=0, concat_axis=0, tiled=True)


def in_order(blocks, dim):
    lengths = list(blocks.shape[1:])
    lengths[dim] *= blocks.shape[0]
    return jnp.moveaxis(blocks, 0, dim).reshape(lengths)


def gather_directly(x, axis, dim):
    blocks = sent_to_all(x, axis)
    return in_order(blocks, dim)


def split_up(x, dim, size):
    before, after = (x.shape[:dim], x.shape[dim + 1 :])
    return jnp.moveaxis(x.reshape(*before, size, -1, *after), dim, 0)


def summed_on_arrival(x, axis, dim):
    blocks = split_up(x, dim, lax.axis_size(axis))
    arrived = lax.all_to_all(blocks, axis, split_axis=0, concat_axis=0, tiled=True)
    return arrived.astype(jnp.float32).sum(axis=0)


def on_device(
    grid_field,
    band_points,
    block_ids,
    block_count,
    block_weight,
    embed_weight,
    edge_src,
    edge_dst,
    edge_in_weight,
    edge_out_weight,
    node_in_weight,
    node_out_weight,
):
    band_index = lax.axis_index("band")
    channels, points = grid_field.shape
    kblocks = block_weight.shape[1]
    node_count = block_weight.shape[2]
    block_len = block_weight.shape[3]
    sub_count = points // block_len
    column = lax.broadcasted_iota(jnp.int32, (1, points), 1)
    live = jnp.where(column < band_points[0], grid_field, jnp.zeros_like(grid_field))
    share = channels // lax.axis_size("ch")
    local_live = lax.dynamic_slice_in_dim(live, lax.axis_index("ch") * share, share, 0)
    extended = extended_2(local_live, (("band", 1),), points // 2)
    first_block = band_index * sub_count - sub_count // 2
    ext_blocks = extended.shape[1] // block_len
    tiles = extended.reshape(extended.shape[0], ext_blocks, block_len)
    local_ids = block_ids[0] - first_block
    tile_ids = lax.broadcasted_iota(jnp.int32, (kblocks, ext_blocks), 1)
    slot_live = lax.broadcasted_iota(jnp.int32, (kblocks, ext_blocks), 0) < block_count[0]
    selector = ((local_ids[:, None] == tile_ids) & slot_live).astype(jnp.bfloat16)
    blocks = jnp.einsum("ks,csp->kcp", selector, tiles, preferred_element_type=jnp.float32).astype(
        jnp.bfloat16
    )
    remapped = jnp.einsum(
        "knp,kcp->nc", block_weight[0], blocks, preferred_element_type=jnp.float32
    ).astype(jnp.bfloat16)
    remapped = gather_directly(remapped, "ch", 1)
    initial = jnp.dot(remapped, embed_weight, preferred_element_type=jnp.float32).astype(
        jnp.bfloat16
    )
    shard_part = lax.all_gather(initial, "ch", axis=1, tiled=True)
    rows_src = edge_in_weight[0]
    rows_dst = edge_in_weight[1]
    rows_node = node_in_weight[0]
    source_acc = jnp.dot(shard_part, rows_src, preferred_element_type=jnp.float32)
    target_acc = jnp.dot(shard_part, rows_dst, preferred_element_type=jnp.float32)
    direct = jnp.dot(shard_part, rows_node, preferred_element_type=jnp.float32)
    source_proj = source_acc.astype(jnp.bfloat16)
    target_proj = target_acc.astype(jnp.bfloat16)
    source_ext = extended_2(source_proj, (("band", 0),), node_count)
    src_local = edge_src - (band_index - 1) * node_count
    dst_local = edge_dst - band_index * node_count
    pre_act = jnp.take(source_ext, src_local, axis=0).astype(jnp.float32) + jnp.take(
        target_proj, dst_local, axis=0
    ).astype(jnp.float32)
    edge_hidden = jax.nn.silu(pre_act).astype(jnp.bfloat16)
    messages = jnp.dot(edge_hidden, edge_out_weight, preferred_element_type=jnp.float32)
    node_ids = lax.broadcasted_iota(jnp.int32, (node_count, 1), 0)
    onehot = (dst_local[None, :] == node_ids).astype(jnp.float32)
    partial_agg = jnp.dot(onehot, messages, preferred_element_type=jnp.float32)
    agg_half = summed_on_arrival(partial_agg.astype(jnp.bfloat16), "ch", 1).astype(jnp.bfloat16)
    rows_agg = node_in_weight[1]
    from_agg = jnp.dot(
        gather_directly(agg_half, "ch", 1), rows_agg, preferred_element_type=jnp.float32
    )
    update = jax.nn.silu(direct + from_agg).astype(jnp.bfloat16)
    partial_out = jnp.dot(update, node_out_weight, preferred_element_type=jnp.float32)
    summed = summed_on_arrival(partial_out.astype(jnp.bfloat16), "ch", 1)
    return (initial.astype(jnp.float32) + summed).astype(jnp.bfloat16)


def solution(mesh):
    return jax.shard_map(
        on_device,
        mesh=mesh,
        in_specs=(
            P(None, "band"),
            P("band"),
            P("band", None),
            P("band"),
            P("band", None, None, None),
            P(None, "ch"),
            P("band"),
            P("band"),
            P(None, None, "ch"),
            P("ch", None),
            P(None, None, "ch"),
            P("ch", None),
        ),
        out_specs=P("band", "ch"),
        check_vma=False,
    )
```

profile of v0, /device:TPU:127, one launch (start us, length us, event | category | flops | bytes accessed | tf_op | source)
XLA Modules:
  0.0 141.0 jit_solution(9254778661560007322)
XLA Ops:
  0.8 2.1 %dynamic-slice_select_fusion = bf16[50,16384]{1,0:T(8,128)(2,1)S(1)} fusion(bf16[100,16384]{1,0:T(8,128)(2,1)} %param.12, s32[]{:T(128)S(6)} %select_n.25, pred[16384]{0:T(1024)(128)(4,1)S(1)} %iota_compare_fusion.4), kind=kLoop, calls=%fused_computation.18 | loop fusion | flops 819200 | bytes 3293188 | tf_op jit(solution)/shard_map/jit(_where)/select_n | solution.py:68
  2.9 1.4 fusion.62
  4.2 4.3 %collective-permute-start = (bf16[50,8192]{1,0:T(8,128)(2,1)}, bf16[50,8192]{1,0:T(8,128)(2,1)}, u32[]{:S(2)}, u32[]{:S(2)}) collective-permute-start(bf16[50,8192]{1,0:T(8,128)(2,1)} %get-tuple-element.7), channel_id=1, source_target_pairs={{0,2},{2,4},{4,6},{6,8},{8,10},{10,12},{12,14},{14,16},{16,18},{18... | collective-permute-start | bytes 2457608 | tf_op jit(solution)/shard_map/ppermute | solution.py:12
  8.6 1.9 %collective-permute-start.1 = (bf16[50,8192]{1,0:T(8,128)(2,1)}, bf16[50,8192]{1,0:T(8,128)(2,1)}, u32[]{:S(2)}, u32[]{:S(2)}) collective-permute-start(bf16[50,8192]{1,0:T(8,128)(2,1)} %get-tuple-element.8), channel_id=1, source_target_pairs={{2,0},{4,2},{6,4},{8,6},{10,8},{12,10},{14,12},{16,14},{18,16},{20... | collective-permute-start | bytes 2457608 | tf_op jit(solution)/shard_map/ppermute | solution.py:15
  11.3 16.5 %collective-permute-done = bf16[50,8192]{1,0:T(8,128)(2,1)} collective-permute-done((bf16[50,8192]{1,0:T(8,128)(2,1)}, bf16[50,8192]{1,0:T(8,128)(2,1)}, u32[]{:S(2)}, u32[]{:S(2)}) %collective-permute-start) | collective-permute-done | bytes 819232 | tf_op jit(solution)/shard_map/ppermute | solution.py:12
  27.8 9.3 %collective-permute-done.1 = bf16[50,8192]{1,0:T(8,128)(2,1)} collective-permute-done((bf16[50,8192]{1,0:T(8,128)(2,1)}, bf16[50,8192]{1,0:T(8,128)(2,1)}, u32[]{:S(2)}, u32[]{:S(2)}) %collective-permute-start.1) | collective-permute-done | bytes 819232 | tf_op jit(solution)/shard_map/ppermute | solution.py:15
  37.1 1.7 %pad_maximum_fusion = bf16[50,32768]{1,0:T(8,128)(2,1)S(1)} fusion(bf16[50,8192]{1,0:T(8,128)(2,1)} %collective-permute-done.1, bf16[50,16384]{1,0:T(8,128)(2,1)S(1)} %dynamic-slice_select_fusion, bf16[50,8192]{1,0:T(8,128)(2,1)} %collective-permute-done), kind=kLoop, calls=%fused_computation.13 | loop fusion | flops 9830400 | bytes 6553600 | tf_op jit(solution)/shard_map/concatenate | solution.py:16
  38.8 1.4 copy.22
  41.0 1.6 %fusion.32 = bf16[256,50]{0,1:T(8,128)(2,1)S(1)} fusion(bf16[1,16,256,512]{3,2,1,0:T(8,128)(2,1)S(1)} %copy-done.1, bf16[16,50,512]{2,0,1:T(8,128)(2,1)S(1)} %fusion.20), kind=kOutput, calls=%fused_computation.28 | convolution fusion | flops 209728000 | bytes 5039104 | tf_op jit(solution)/shard_map/knp,kcp->nc/dot_general | solution.py:82
  42.6 5.3 %all_to_all.20 = bf16[2,256,50]{1,2,0:T(8,128)(2,1)S(1)} all-to-all(bf16[2,256,50]{1,2,0:T(8,128)(2,1)S(1)} %broadcast_in_dim.43), channel_id=1, replica_groups=mesh['band'=128,'ch'=2] {'ch'}, dimensions={0} | all-to-all | bytes 102400 | tf_op jit(solution)/shard_map/all_to_all | solution.py:22
  48.2 2.2 %all_gather.3 = bf16[256,1024]{1,0:T(8,128)(2,1)S(1)} all-gather(bf16[256,512]{1,0:T(8,128)(2,1)S(1)} %convolution_convert_fusion.3), channel_id=1, replica_groups=mesh['band'=128,'ch'=2] {'ch'}, dimensions={1}, use_global_device_ids=true | all-gather | bytes 786432 | tf_op jit(solution)/shard_map/all_gather | solution.py:89
  50.4 1.7 %convolution_convert_fusion.2 = bf16[256,512]{1,0:T(8,128)(2,1)S(1)} fusion(bf16[256,1024]{1,0:T(8,128)(2,1)S(1)} %all_gather.3, bf16[2,1024,512]{2,1,0:T(8,128)(2,1)} %param.20), kind=kOutput, calls=%fused_computation.24 | convolution fusion | flops 268566528 | bytes 1835008 | tf_op jit(solution)/shard_map/dot_general | solution.py:93
  52.0 1.7 %convolution_convert_fusion.1 = bf16[256,512]{1,0:T(8,128)(2,1)S(1)} fusion(bf16[256,1024]{1,0:T(8,128)(2,1)S(1)} %all_gather.3, bf16[2,1024,512]{2,1,0:T(8,128)(2,1)} %param.20), kind=kOutput, calls=%fused_computation.23 | convolution fusion | flops 268566528 | bytes 1835008 | tf_op jit(solution)/shard_map/dot_general | solution.py:94
  53.7 1.9 %collective-permute-start.3 = (bf16[256,512]{1,0:T(8,128)(2,1)S(1)}, bf16[256,512]{1,0:T(8,128)(2,1)S(1)}, u32[]{:S(2)}, u32[]{:S(2)}) collective-permute-start(bf16[256,512]{1,0:T(8,128)(2,1)S(1)} %convolution_convert_fusion.2), channel_id=1, source_target_pairs={{2,0},{4,2},{6,4},{8,6},{10,8},{12,10},{14,12},{16,14},{18,16},{20... | collective-permute-start | bytes 786440 | tf_op jit(solution)/shard_map/ppermute | solution.py:15
  55.6 9.0 %collective-permute-start.2 = (bf16[256,512]{1,0:T(8,128)(2,1)S(1)}, bf16[256,512]{1,0:T(8,128)(2,1)S(1)}, u32[]{:S(2)}, u32[]{:S(2)}) collective-permute-start(bf16[256,512]{1,0:T(8,128)(2,1)S(1)} %convolution_convert_fusion.2), channel_id=1, source_target_pairs={{0,2},{2,4},{4,6},{6,8},{8,10},{10,12},{12,14},{14,16},{16,18},{18... | collective-permute-start | bytes 786440 | tf_op jit(solution)/shard_map/ppermute | solution.py:12
  64.6 21.4 %gather_fusion.1 = bf16[5120,512]{1,0:T(8,128)(2,1)} fusion(bf16[256,512]{1,0:T(8,128)(2,1)S(1)} %convolution_convert_fusion.1, s32[5120]{0:T(1024)S(1)} %fusion.50), kind=kCustom, calls=%fused_computation.1 | custom fusion | bytes 10506240 | tf_op jit(solution)/shard_map/jit(_take)/gather | solution.py:101
  86.0 2.5 %fusion.38 = f32[256,512]{1,0:T(8,128)} fusion(bf16[256,1024]{1,0:T(8,128)(2,1)S(1)} %all_gather.3, bf16[2,1024,512]{2,1,0:T(8,128)(2,1)} %param.22), kind=kOutput, calls=%fused_computation.32 | convolution fusion | flops 268435456 | bytes 2097152 | tf_op jit(solution)/shard_map/dot_general | solution.py:95
  88.5 21.4 %gather_fusion = bf16[5120,512]{1,0:T(8,128)(2,1)} fusion(bf16[768,512]{1,0:T(8,128)(2,1)S(1)} %pad_maximum_fusion.1, s32[5120]{0:T(1024)S(1)} %fusion.51), kind=kCustom, calls=%fused_computation | custom fusion | bytes 10506240 | tf_op jit(solution)/shard_map/jit(_take)/gather | solution.py:101
  109.9 14.5 %fusion.23 = bf16[256,1024]{1,0:T(8,128)(2,1)S(1)} fusion(bf16[512,1024]{1,0:T(8,128)(2,1)S(1)} %copy-done, bf16[5120,512]{1,0:T(8,128)(2,1)} %gather_fusion.1, bf16[5120,512]{1,0:T(8,128)(2,1)} %gather_fusion, pred[5120]{0:T(1024)(128)(4,1)S(1)} %get-tuple-element.5, pred[5120]{0:T(1024)(128)(4,1)S(1)} %get-tuple-element.9, s32[5120]{0:T(1024)S(1)} %get-tuple-element.6), kind=kOutput, calls=%fused_computation.21 | convolution fusion | flops 8080850944 | bytes 12089344 | tf_op jit(solution)/shard_map/dot_general | solution.py:108
  124.4 4.8 %all_to_all.21 = bf16[2,256,512]{2,1,0:T(8,128)(2,1)S(1)} all-to-all(bf16[2,256,512]{2,1,0:T(8,128)(2,1)S(1)} %bitcast.75), channel_id=1, replica_groups=mesh['band'=128,'ch'=2] {'ch'}, dimensions={0} | all-to-all | bytes 1048576 | tf_op jit(solution)/shard_map/all_to_all | solution.py:43
  129.5 4.2 %all_to_all.22 = bf16[2,256,512]{1,2,0:T(8,128)(2,1)S(1)} all-to-all(bf16[2,256,512]{1,2,0:T(8,128)(2,1)S(1)} %broadcast_in_dim.49), channel_id=1, replica_groups=mesh['band'=128,'ch'=2] {'ch'}, dimensions={0} | all-to-all | bytes 1048576 | tf_op jit(solution)/shard_map/all_to_all | solution.py:22
  133.7 2.3 %convolution_convert_fusion = bf16[256,1024]{1,0:T(8,128)(2,1)S(1)} fusion(bf16[512,1024]{1,0:T(8,128)(2,1)S(1)} %copy-done.5, f32[256,512]{1,0:T(8,128)} %fusion.38, bf16[256,1024]{0,1:T(8,128)(2,1)S(1)} %bitcast.78, bf16[2,1024,512]{2,1,0:T(8,128)(2,1)} %param.22), kind=kOutput, calls=%fused_computation.20 | convolution fusion | flops 537919488 | bytes 3670016 | tf_op jit(solution)/shard_map/dot_general | solution.py:115
  136.0 4.2 %all_to_all.23 = bf16[2,256,512]{2,1,0:T(8,128)(2,1)S(1)} all-to-all(bf16[2,256,512]{2,1,0:T(8,128)(2,1)S(1)} %bitcast.76), channel_id=1, replica_groups=mesh['band'=128,'ch'=2] {'ch'}, dimensions={0} | all-to-all | bytes 1048576 | tf_op jit(solution)/shard_map/all_to_all | solution.py:43
  140.2 0.8 add_convert_fusion
  (33 shorter events, 1.6 us)
Async XLA Ops:
  0.0 109.9 %copy-start = (bf16[512,1024]{1,0:T(8,128)(2,1)S(1)}, bf16[512,1024]{1,0:T(8,128)(2,1)}, u32[]{:S(2)}) copy-start(bf16[512,1024]{1,0:T(8,128)(2,1)} %param.21) | copy-start | bytes 3145732
  0.0 10.5 %copy-start.6 = (s32[1,16]{1,0:T(1,128)S(1)}, s32[1,16]{1,0:T(1,128)}, u32[]{:S(2)}) copy-start(s32[1,16]{1,0:T(1,128)} %param.14) | copy-start | bytes 196
  0.0 11.2 %copy-start.3 = (s32[5120]{0:T(1024)S(1)}, s32[5120]{0:T(1024)}, u32[]{:S(2)}) copy-start(s32[5120]{0:T(1024)} %param.18) | copy-start | bytes 61444
  0.0 11.2 %copy-start.4 = (s32[5120]{0:T(1024)S(1)}, s32[5120]{0:T(1024)}, u32[]{:S(2)}) copy-start(s32[5120]{0:T(1024)} %param.19) | copy-start | bytes 61444
  4.2 23.6 %collective-permute-start = (bf16[50,8192]{1,0:T(8,128)(2,1)}, bf16[50,8192]{1,0:T(8,128)(2,1)}, u32[]{:S(2)}, u32[]{:S(2)}) collective-permute-start(bf16[50,8192]{1,0:T(8,128)(2,1)} %get-tuple-element.7), channel_id=1, source_target_pairs={{0,2},{2,4},{4,6},{6,8},{8,10},{10,12},{12,14},{14,16},{16,18},{18... | collective-permute-start | bytes 2457608 | tf_op jit(solution)/shard_map/ppermute | solution.py:12
  8.6 28.5 %collective-permute-start.1 = (bf16[50,8192]{1,0:T(8,128)(2,1)}, bf16[50,8192]{1,0:T(8,128)(2,1)}, u32[]{:S(2)}, u32[]{:S(2)}) collective-permute-start(bf16[50,8192]{1,0:T(8,128)(2,1)} %get-tuple-element.8), channel_id=1, source_target_pairs={{2,0},{4,2},{6,4},{8,6},{10,8},{12,10},{14,12},{16,14},{18,16},{20... | collective-permute-start | bytes 2457608 | tf_op jit(solution)/shard_map/ppermute | solution.py:15
  38.8 2.2 %copy-start.1 = (bf16[1,16,256,512]{3,2,1,0:T(8,128)(2,1)S(1)}, bf16[1,16,256,512]{3,2,1,0:T(8,128)(2,1)}, u32[]{:S(2)}) copy-start(bf16[1,16,256,512]{3,2,1,0:T(8,128)(2,1)} %param.16) | copy-start | bytes 12582916
  40.2 7.7 %copy-start.2 = (bf16[100,512]{1,0:T(8,128)(2,1)S(1)}, bf16[100,512]{1,0:T(8,128)(2,1)}, u32[]{:S(2)}) copy-start(bf16[100,512]{1,0:T(8,128)(2,1)} %param.17) | copy-start | bytes 307204
  53.7 34.8 %collective-permute-start.3 = (bf16[256,512]{1,0:T(8,128)(2,1)S(1)}, bf16[256,512]{1,0:T(8,128)(2,1)S(1)}, u32[]{:S(2)}, u32[]{:S(2)}) collective-permute-start(bf16[256,512]{1,0:T(8,128)(2,1)S(1)} %convolution_convert_fusion.2), channel_id=1, source_target_pairs={{2,0},{4,2},{6,4},{8,6},{10,8},{12,10},{14,12},{16,14},{18,16},{20... | collective-permute-start | bytes 786440 | tf_op jit(solution)/shard_map/ppermute | solution.py:15
  55.6 32.8 %collective-permute-start.2 = (bf16[256,512]{1,0:T(8,128)(2,1)S(1)}, bf16[256,512]{1,0:T(8,128)(2,1)S(1)}, u32[]{:S(2)}, u32[]{:S(2)}) collective-permute-start(bf16[256,512]{1,0:T(8,128)(2,1)S(1)} %convolution_convert_fusion.2), channel_id=1, source_target_pairs={{0,2},{2,4},{4,6},{6,8},{8,10},{10,12},{12,14},{14,16},{16,18},{18... | collective-permute-start | bytes 786440 | tf_op jit(solution)/shard_map/ppermute | solution.py:12
  124.4 9.3 %copy-start.5 = (bf16[512,1024]{1,0:T(8,128)(2,1)S(1)}, bf16[512,1024]{1,0:T(8,128)(2,1)}, u32[]{:S(2)}) copy-start(bf16[512,1024]{1,0:T(8,128)(2,1)} %param.23) | copy-start | bytes 3145732
where the time goes:
time: 142 us; the launch traced here: 141 us
  local copies, waits for them, and re-layouts  46 us (32%)
  waiting for transfers between devices  25.8 us (18%)
  matrix products  24.9 us (18%)
  blocking collectives  20.6 us (15%)
  starting transfers between devices  17.1 us (12%)
  other arithmetic  4.87 us (3%)
  between operations  1.67 us (1%)
    gather x1, local copies, waits for them, and re-layouts, on_device(): jnp.take(target_proj, dst_local, axis=0).astype(jnp.float32)  21.4 us
    gather x1, local copies, waits for them, and re-layouts, on_device(): jnp.take(source_ext, src_local, axis=0).astype(jnp.float32)  21.4 us
    ppermute x2, waiting for transfers between devices, extended_2(): lax.ppermute(lax.slice_in_dim(block, block.shape[dim] - width, None, axis...  16.5 us
    dot_general x1, matrix products, on_device(): partial_agg = jnp.dot(onehot, messages, preferred_element_type=jnp.float32)  14.5 us
    ppermute x2, starting transfers between devices, extended_2(): lax.ppermute(lax.slice_in_dim(block, block.shape[dim] - width, None, axis...  13.3 us
    all_to_all x2, blocking collectives, sent_to_all(): return lax.all_to_all(copies, axis, split_axis=0, concat_axis=0, tiled=True)  9.49 us
    ppermute x2, waiting for transfers between devices, extended_2(): lax.ppermute(lax.slice_in_dim(block, 0, width, axis=dim), axis, backward)  9.27 us
    all_to_all x2, blocking collectives, summed_on_arrival(): lax.all_to_all(blocks, axis, split_axis=0, concat_axis=0, tiled=True)  8.97 us
  transfers between devices with their start and end apart: 4, of which 2 were waited for; matrix products, arithmetic and copies ran while one was open for 17% of the time, Pallas kernels for 0%

commit v1 on v0

v1 whole, which is shorter than its diff:
```python
import functools

import jax
import jax.numpy as jnp
from jax import lax
from jax.experimental import pallas as pl
from jax.experimental.pallas import tpu as pltpu
from jax.sharding import PartitionSpec as P

F32 = jnp.float32
BF16 = jnp.bfloat16
LANES = 128
VMEM = pl.BlockSpec(memory_space=pltpu.VMEM)
SMEM = pl.BlockSpec(memory_space=pltpu.SMEM)
NT = (((1,), (1,)), ((), ()))
TN = (((0,), (0,)), ((), ()))


def silu(v):
    return v * (0.5 * jnp.tanh(0.5 * v) + 0.5)


def remap_kernel(own, where_ref, ids_ref, count_ref, limit_ref, weight_ref, points_ref, *rest):
    out_ref = rest[-1]
    band, core = where_ref[0], where_ref[1]
    channels = points_ref.shape[0]
    kblocks, _, block_len = weight_ref.shape
    blocks = points_ref.shape[1] // block_len
    if own:
        sub_count = blocks
        out_ref[...] = jnp.zeros_like(out_ref)
    else:
        sub_count = 2 * blocks
        out_ref[...] = rest[0][...]
    for k in range(kblocks):
        local = ids_ref[0, k] - band * sub_count
        live = k < count_ref[0]
        if own:
            mine = (local >= 0) & (local < sub_count) & (core == k % 2)
            block = local
        else:
            low = (core == 0) & (local < 0)
            high = (core == 1) & (local >= sub_count)
            mine = low | high
            block = jnp.where(low, local + blocks, local - sub_count)
        block = jnp.clip(block, 0, blocks - 1)

        @pl.when(live & mine)
        def _():
            at = pl.multiple_of(block * block_len, block_len)
            x = points_ref[:, pl.ds(at, block_len)]
            if own:
                column = at + lax.broadcasted_iota(jnp.int32, x.shape, 1)
                x = jnp.where(column < limit_ref[0], x, jnp.zeros_like(x))
            out_ref[:channels, :] += lax.dot_general(
                x, weight_ref[k], NT, preferred_element_type=F32
            )


def edge_kernel(where_ref, low_ref, mid_ref, high_ref, into_ref, src_ref, dst_ref, out_ref, acc_ref):
    band = where_ref[0]
    nodes = mid_ref.shape[1]
    chunks, size = src_ref.shape
    sources = jnp.concatenate([low_ref[...], mid_ref[...], high_ref[...]], axis=0)
    acc_ref[...] = jnp.zeros_like(acc_ref)

    def step(i, carry):
        src = src_ref[pl.ds(i, 1), :] - (band - 1) * nodes
        dst = dst_ref[pl.ds(i, 1), :] - band * nodes
        piece = src // nodes
        src = src - piece * nodes
        node = lax.broadcasted_iota(jnp.int32, (nodes, size), 0)
        from_hot = (node == src).astype(F32).astype(BF16)
        to_hot = (node == dst).astype(F32).astype(BF16)
        got = jnp.dot(sources, from_hot, preferred_element_type=F32)
        a, b, c = got[:LANES], got[LANES : 2 * LANES], got[2 * LANES :]
        from_src = jnp.where(piece == 0, a, jnp.where(piece == 1, b, c))
        from_dst = jnp.dot(mid_ref[...], to_hot, preferred_element_type=F32)
        both = jnp.concatenate([from_src.astype(BF16), from_dst.astype(BF16)], axis=0)
        pre = jnp.dot(into_ref[...], both, preferred_element_type=F32)
        hidden = silu(pre).astype(BF16)
        acc_ref[...] += lax.dot_general(to_hot, hidden, NT, preferred_element_type=F32)
        return carry

    lax.fori_loop(0, chunks, step, 0)
    out_ref[...] = acc_ref[...].astype(out_ref.dtype)


def update_kernel(where_ref, sums_ref, own_ref, other_ref, mid_ref, direct_ref, out_ref):
    core = where_ref[1]
    v = jnp.dot(sums_ref[core], own_ref[...], preferred_element_type=F32)
    v += jnp.dot(sums_ref[1 - core], other_ref[...], preferred_element_type=F32)
    v += lax.dot_general(mid_ref[...], direct_ref[...], TN, preferred_element_type=F32)
    out_ref[...] = silu(v).astype(out_ref.dtype)


def result_kernel(where_ref, update_ref, own_ref, other_ref, mid_ref, embed_ref, out_ref):
    core = where_ref[1]
    v = jnp.dot(update_ref[core], own_ref[...], preferred_element_type=F32)
    v += jnp.dot(update_ref[1 - core], other_ref[...], preferred_element_type=F32)
    v += lax.dot_general(mid_ref[...], embed_ref[...], TN, preferred_element_type=F32)
    out_ref[...] = v.astype(out_ref.dtype)


def call(kernel, out, specs, limit_mib, flops, args, scratch=()):
    return pl.pallas_call(
        kernel,
        out_shape=out,
        in_specs=specs,
        out_specs=VMEM,
        scratch_shapes=list(scratch),
        compiler_params=pltpu.CompilerParams(vmem_limit_bytes=limit_mib << 20),
        cost_estimate=pl.CostEstimate(flops=flops, bytes_accessed=1 << 20, transcendentals=0),
    )(*args)


def on_device(
    grid_field,
    band_points,
    block_ids,
    block_count,
    block_weight,
    embed_weight,
    edge_src,
    edge_dst,
    edge_in_weight,
    edge_out_weight,
    node_in_weight,
    node_out_weight,
):
    bands = lax.axis_size("band")
    band, core = lax.axis_index("band"), lax.axis_index("ch")
    where = jnp.stack([band, core]).astype(jnp.int32)
    channels, points = grid_field.shape
    _, kblocks, nodes, block_len = block_weight.shape
    share = embed_weight.shape[1]
    half = points // 2
    weight = block_weight[0]

    start = (1 - core) * half
    piece = lax.dynamic_slice_in_dim(grid_field, start, half, 1)
    column = start + lax.broadcasted_iota(jnp.int32, (1, half), 1)
    piece = jnp.where(column < band_points[0], piece, jnp.zeros_like(piece))
    pairs = [(2 * b, 2 * b + 2) for b in range(bands - 1)]
    pairs += [(2 * b + 3, 2 * b + 1) for b in range(bands - 1)]
    halo = lax.ppermute(piece, ("band", "ch"), pairs)

    swap = [(0, 1), (1, 0)]
    embed_full = lax.all_gather(embed_weight, "ch", axis=1, tiled=True)
    out_other = lax.ppermute(edge_out_weight, "ch", swap)
    mine = core * share
    last_own = lax.dynamic_slice_in_dim(node_out_weight, mine, share, 1)
    last_other = lax.ppermute(
        lax.dynamic_slice_in_dim(node_out_weight, share - mine, share, 1), "ch", swap
    )

    def into(w):
        return lax.dot_general(
            w, embed_full, (((0,), (1,)), ((), ())), preferred_element_type=F32
        ).astype(BF16)

    pad = ((0, 0), (0, LANES - channels))
    into_edge = jnp.concatenate(
        [jnp.pad(into(edge_in_weight[0]), pad), jnp.pad(into(edge_in_weight[1]), pad)], axis=1
    )
    direct = jnp.dot(embed_full, node_in_weight[0], preferred_element_type=F32).astype(BF16)
    direct = jnp.pad(direct, (pad[1], pad[0]))
    embed_pad = jnp.pad(embed_weight, (pad[1], pad[0]))
    agg_own = jnp.dot(edge_out_weight, node_in_weight[1], preferred_element_type=F32).astype(BF16)
    agg_other = jnp.dot(out_other, node_in_weight[1], preferred_element_type=F32).astype(BF16)

    sums = jax.ShapeDtypeStruct((LANES, nodes), F32)
    remap_flops = 2 * channels * nodes * block_len * kblocks // 4
    partial = call(
        functools.partial(remap_kernel, True),
        sums,
        [SMEM] * 4 + [VMEM] * 2,
        12,
        remap_flops,
        (where, block_ids, block_count, band_points, weight, grid_field),
    )
    partial = call(
        functools.partial(remap_kernel, False),
        sums,
        [SMEM] * 4 + [VMEM] * 3,
        12,
        remap_flops,
        (where, block_ids, block_count, band_points, weight, halo, partial),
    )
    mid = lax.all_gather(partial, "ch").sum(axis=0).astype(BF16)
    upward = [(b, b + 1) for b in range(bands - 1)]
    low = lax.ppermute(mid, "band", upward)
    high = lax.ppermute(mid, "band", [(t, s) for s, t in upward])

    edges = edge_src.shape[0]
    size = 1024
    by_node = call(
        edge_kernel,
        jax.ShapeDtypeStruct((nodes, share), BF16),
        [SMEM] + [VMEM] * 6,
        20,
        2 * edges * nodes * 7 * 256,
        (
            where,
            low,
            mid,
            high,
            into_edge,
            edge_src.reshape(edges // size, size),
            edge_dst.reshape(edges // size, size),
        ),
        [pltpu.VMEM((nodes, share), F32)],
    )
    by_node = lax.all_gather(by_node, "ch")
    update = call(
        update_kernel,
        jax.ShapeDtypeStruct((nodes, share), BF16),
        [SMEM] + [VMEM] * 5,
        8,
        2 * nodes * share * 2 * share,
        (where, by_node, agg_own, agg_other, mid, direct),
    )
    update = lax.all_gather(update, "ch")
    return call(
        result_kernel,
        jax.ShapeDtypeStruct((nodes, share), BF16),
        [SMEM] + [VMEM] * 5,
        8,
        2 * nodes * share * 2 * share,
        (where, update, last_own, last_other, mid, embed_pad),
    )


def solution(mesh):
    return jax.shard_map(
        on_device,
        mesh=mesh,
        in_specs=(
            P(None, "band"),
            P("band"),
            P("band", None),
            P("band"),
            P("band", None, None, None),
            P(None, "ch"),
            P("band"),
            P("band"),
            P(None, None, "ch"),
            P("ch", None),
            P(None, None, "ch"),
            P("ch", None),
        ),
        out_specs=P("band", "ch"),
        check_vma=False,
    )
```

time: 142 us -> 69.4 us (0.49)
  local copies, waits for them, and re-layouts: 46 us -> 9.83 us
  matrix products: 24.9 us -> 6.42 us
  waiting for transfers between devices: 25.8 us -> 11 us
  Pallas kernels: 0 us -> 13.4 us
  blocking collectives: 20.6 us -> 9.99 us
  starting transfers between devices: 17.1 us -> 13.3 us
  other arithmetic: 4.87 us -> 3.31 us
    gather x2 -> x0, local copies, waits for them, and re-layouts: 42.7 us -> none  [the longest x1 21.4 us: on_device(): jnp.take(target_proj, dst_local, axis=0).astype(jnp.float32)]
    dot_general x8 -> x5, matrix products: 24.9 us -> 6.42 us  [the longest x2 2.14 us: into(): lax.dot_general(w, embed_full, (((0,), (1,)), ((), ())), preferred_elemen...]
    all_to_all x4 -> x0, blocking collectives: 18.5 us -> none  [the longest x2 9.49 us: sent_to_all(): return lax.all_to_all(copies, axis, split_axis=0, concat_axis=0, tiled=True)]
    ppermute x4 -> x5, waiting for transfers between devices: 25.8 us -> 11 us  [the longest x1 6.53 us: on_device(): high = lax.ppermute(mid, 'band', [(t, s) for s, t in upward])]
    pallas_call x0 -> x5, Pallas kernels: none -> 13.4 us  [call(): pl.pallas_call(kernel, out_shape=out, in_specs=specs, out_specs=VMEM, scr...]
    all_gather x1 -> x4, blocking collectives: 2.18 us -> 9.99 us  [the longest x1 3.73 us: on_device(): by_node = lax.all_gather(by_node, 'ch')]
    ppermute x4 -> x5, starting transfers between devices: 17.1 us -> 13.3 us  [the longest x1 6 us: on_device(): low = lax.ppermute(mid, 'band', upward)]
    unnamed x15 -> x36, local copies, waits for them, and re-layouts: 1.59 us -> 3.67 us
  transfers between devices with their start and end apart: 4 -> 5, of which waited for: 2 -> 2; matrix products, arithmetic and copies ran while one was open for 17% -> 18% of each run, Pallas kernels for 0% -> 16%
where the time goes in v1:
time: 69.4 us; the launch traced here: 68.9 us
  Pallas kernels  13.4 us (19%)
  starting transfers between devices  13.3 us (19%)
  waiting for transfers between devices  11 us (16%)
  blocking collectives  9.99 us (14%)
  local copies, waits for them, and re-layouts  9.83 us (14%)
  matrix products  6.42 us (9%)
  other arithmetic  3.31 us (5%)
  between operations  1.66 us (2%)
    pallas_call x5, Pallas kernels, call(): pl.pallas_call(kernel, out_shape=out, in_specs=specs, out_specs=VMEM, scr...  13.4 us
    ppermute x1, waiting for transfers between devices, on_device(): high = lax.ppermute(mid, 'band', [(t, s) for s, t in upward])  6.53 us
    ppermute x1, starting transfers between devices, on_device(): low = lax.ppermute(mid, 'band', upward)  6 us
    ppermute x1, waiting for transfers between devices, on_device(): halo = lax.ppermute(piece, ('band', 'ch'), pairs)  4.46 us
    all_gather x1, blocking collectives, on_device(): by_node = lax.all_gather(by_node, 'ch')  3.73 us
    unnamed x36, local copies, waits for them, and re-layouts  3.67 us
    select_n x1, other arithmetic, on_device(): piece = jnp.where(column < band_points[0], piece, jnp.zeros_like(piece))  3.15 us
    ppermute x1, starting transfers between devices, on_device(): out_other = lax.ppermute(edge_out_weight, 'ch', swap)  2.91 us
  transfers between devices with their start and end apart: 5, of which 2 were waited for; matrix products, arithmetic and copies ran while one was open for 18% of the time, Pallas kernels for 16%

profile of v1, /device:TPU:127, one launch (start us, length us, event | category | flops | bytes accessed | tf_op | source)
XLA Modules:
  0.0 68.9 jit_solution(10430649217151884673)
XLA Ops:
  0.8 3.2 %dynamic-slice_select_fusion = bf16[100,8192]{1,0:T(8,128)(2,1)} fusion(bf16[100,16384]{1,0:T(8,128)(2,1)} %points_ref.1, s32[]{:T(128)S(6)} %select_n.13, pred[8192]{0:T(1024)(128)(4,1)S(1)} %add_compare_fusion), kind=kLoop, calls=%fused_computation | loop fusion | flops 819200 | bytes 3284996 | tf_op jit(solution)/shard_map/jit(_where)/select_n | solution.py:143
  3.9 2.4 %collective-permute-start = (bf16[100,8192]{1,0:T(8,128)(2,1)}, bf16[100,8192]{1,0:T(8,128)(2,1)}, u32[]{:S(2)}, u32[]{:S(2)}) collective-permute-start(bf16[100,8192]{1,0:T(8,128)(2,1)} %dynamic-slice_select_fusion), channel_id=1, source_target_pairs={{0,2},{2,4},{4,6},{6,8},{8,10},{10,12},{12,14},{14,16},{16,18},{18... | collective-permute-start | bytes 4915208 | tf_op jit(solution)/shard_map/ppermute | solution.py:146
  6.4 2.9 %collective-permute-start.3 = (bf16[512,1024]{1,0:T(8,128)(2,1)}, bf16[512,1024]{1,0:T(8,128)(2,1)}, u32[]{:S(2)}, u32[]{:S(2)}) collective-permute-start(bf16[512,1024]{1,0:T(8,128)(2,1)} %param.21), channel_id=1, source_target_pairs={{0,1},{1,0},{2,3},{3,2},{4,5},{5,4},{6,7},{7,6},{8,9},{9,8},{10,11... | collective-permute-start | bytes 3145736 | tf_op jit(solution)/shard_map/ppermute | solution.py:150
  9.3 1.1 %constant_dynamic-slice_fusion = (bf16[512,512]{1,0:T(8,128)(2,1)}, bf16[512,512]{1,0:T(8,128)(2,1)}) fusion(bf16[512,1024]{1,0:T(8,128)(2,1)S(1)} %copy-done.8, s32[]{:T(128)S(6)} %select_n.16, s32[]{:T(128)S(6)} %select_n.15), kind=kLoop, calls=%fused_computation.22 | loop fusion | bytes 2097160 | tf_op jit(solution)/shard_map/dynamic_slice | solution.py:154
  11.1 2.1 %all_gather.23 = bf16[100,1024]{1,0:T(8,128)(2,1)S(1)} all-gather(bf16[100,512]{1,0:T(8,128)(2,1)S(1)} %copy-done.11), channel_id=1, replica_groups=mesh['band'=128,'ch'=2] {'ch'}, dimensions={1}, use_global_device_ids=true | all-gather | bytes 307200 | tf_op jit(solution)/shard_map/all_gather | solution.py:149
  15.0 1.8 %convolution_convert_fusion.3 = bf16[512,100]{0,1:T(8,128)(2,1)S(1)} fusion(bf16[100,1024]{1,0:T(8,128)(2,1)} %copy-done.12, bf16[2,1024,512]{2,1,0:T(8,128)(2,1)} %param.20), kind=kOutput, calls=%fused_computation.4 | convolution fusion | flops 104908800 | bytes 1363968 | tf_op jit(solution)/shard_map/dot_general | solution.py:158
  16.8 0.8 %copy.16 = bf16[512,100]{1,0:T(8,128)(2,1)} copy(bf16[512,100]{0,1:T(8,128)(2,1)S(1)} %convolution_convert_fusion.3) | data formatting | bytes 204800 | tf_op jit(solution)/shard_map/convert_element_type | solution.py:160
  18.2 1.3 %reshape.14.dst_ref = s32[5,1024]{1,0:T(8,128)} reshape(s32[5120]{0:T(1024)} %param.19) | data formatting | bytes 40960 | tf_op jit(solution)/shard_map/reshape | solution.py:210
  19.6 0.9 %pad.17.embed_ref = bf16[128,512]{1,0:T(8,128)(2,1)S(1)} pad(bf16[100,512]{1,0:T(8,128)(2,1)} %param.17, bf16[]{:T(256)} %constant.22.clone.1), padding=0_28x0_0 | pad | bytes 233474 | tf_op jit(solution)/shard_map/jit(_pad)/pad | solution.py:168
  20.5 1.6 %convolution_convert_fusion.2 = bf16[100,512]{1,0:T(8,128)(2,1)S(1)} fusion(bf16[100,1024]{1,0:T(8,128)(2,1)} %copy-done.12, bf16[2,1024,512]{2,1,0:T(8,128)(2,1)} %param.22), kind=kOutput, calls=%fused_computation.3 | convolution fusion | flops 104908800 | bytes 1363968 | tf_op jit(solution)/shard_map/dot_general | solution.py:166
  22.9 2.2 %copy-done = bf16[1,16,256,512]{3,2,1,0:T(8,128)(2,1)S(1)} copy-done((bf16[1,16,256,512]{3,2,1,0:T(8,128)(2,1)S(1)}, bf16[1,16,256,512]{3,2,1,0:T(8,128)(2,1)}, u32[]{:S(2)}) %copy-start) | copy-done | bytes 4194328
  25.1 1.2 %shard_map.118.rest_0_ = f32[128,256]{1,0:T(8,128)S(1)} custom-call(s32[2]{0:T(128)S(1)} %pad_add_fusion.where_ref, s32[1,16]{1,0:T(1,128)S(1)} %copy-done.7, s32[1]{0:T(128)S(6)} %copy.18.count_ref, s32[1]{0:T(128)} %copy.17.limit_ref, bf16[16,256,512]{2,1,0:T(8,128)(2,1)S(1)} %bitcast.27, bf16[100,16384]{1,0:T(8,128)(2,1)S(1)} %copy-done.2), custom_call_target="tpu_custom_call" | custom-call | flops 104857600 | bytes 1048576 | tf_op jit(solution)/shard_map/pallas_call | solution.py:106
  27.8 4.5 %collective-permute-done.points_ref = bf16[100,8192]{1,0:T(8,128)(2,1)} collective-permute-done((bf16[100,8192]{1,0:T(8,128)(2,1)}, bf16[100,8192]{1,0:T(8,128)(2,1)}, u32[]{:S(2)}, u32[]{:S(2)}) %collective-permute-start) | collective-permute-done | bytes 1638432 | tf_op jit(solution)/shard_map/ppermute | solution.py:146
  32.2 2.1 %shard_map.119 = f32[128,256]{1,0:T(8,128)S(1)} custom-call(s32[2]{0:T(128)S(1)} %pad_add_fusion.where_ref, s32[1,16]{1,0:T(1,128)S(1)} %copy-done.7, s32[1]{0:T(128)S(6)} %copy.18.count_ref, s32[1]{0:T(128)} %copy.17.limit_ref, bf16[16,256,512]{2,1,0:T(8,128)(2,1)S(1)} %bitcast.28, bf16[100,8192]{1,0:T(8,128)(2,1)} %collective-permute-done.points_ref, ...), custom_call_target="tpu_custom_call" | custom-call | flops 104857600 | bytes 1048576 | tf_op jit(solution)/shard_map/pallas_call | solution.py:106
  34.4 2.0 %all-gather = f32[256,256]{1,0:T(8,128)S(1)} all-gather(f32[128,256]{1,0:T(8,128)S(1)} %shard_map.119), channel_id=2, replica_groups=mesh['band'=128,'ch'=2] {'ch'}, dimensions={0}, use_global_device_ids=true | all-gather | bytes 393216 | tf_op jit(solution)/shard_map/all_gather | solution.py:190
  36.4 6.0 %collective-permute-start.1 = (bf16[128,256]{1,0:T(8,128)(2,1)S(1)}, bf16[128,256]{1,0:T(8,128)(2,1)S(1)}, u32[]{:S(2)}, u32[]{:S(2)}) collective-permute-start(bf16[128,256]{1,0:T(8,128)(2,1)S(1)} %reduce_sum.9.mid_ref), channel_id=1, source_target_pairs={{0,2},{2,4},{4,6},{6,8},{8,10},{10,12},{12,14},{14,16},{16,18},{18... | collective-permute-start | bytes 196616 | tf_op jit(solution)/shard_map/ppermute | solution.py:192
  42.4 1.9 %collective-permute-start.2 = (bf16[128,256]{1,0:T(8,128)(2,1)S(1)}, bf16[128,256]{1,0:T(8,128)(2,1)S(1)}, u32[]{:S(2)}, u32[]{:S(2)}) collective-permute-start(bf16[128,256]{1,0:T(8,128)(2,1)S(1)} %reduce_sum.9.mid_ref), channel_id=1, source_target_pairs={{2,0},{4,2},{6,4},{8,6},{10,8},{12,10},{14,12},{16,14},{18,16},{20... | collective-permute-start | bytes 196616 | tf_op jit(solution)/shard_map/ppermute | solution.py:193
  44.3 1.9 %convolution_convert_fusion.other_ref = bf16[512,512]{1,0:T(8,128)(2,1)S(1)} fusion(bf16[512,1024]{1,0:T(8,128)(2,1)} %collective-permute-done.3, bf16[2,1024,512]{2,1,0:T(8,128)(2,1)S(1)} %copy-done.16), kind=kOutput, calls=%fused_computation.1 | convolution fusion | flops 537133056 | bytes 2621440 | tf_op jit(solution)/shard_map/dot_general | solution.py:170
  46.3 6.5 %collective-permute-done.2.high_ref = bf16[128,256]{1,0:T(8,128)(2,1)S(1)} collective-permute-done((bf16[128,256]{1,0:T(8,128)(2,1)S(1)}, bf16[128,256]{1,0:T(8,128)(2,1)S(1)}, u32[]{:S(2)}, u32[]{:S(2)}) %collective-permute-start.2) | collective-permute-done | bytes 65568 | tf_op jit(solution)/shard_map/ppermute | solution.py:193
  52.8 6.8 %shard_map.120 = bf16[256,512]{1,0:T(8,128)(2,1)S(1)} custom-call(s32[2]{0:T(128)S(1)} %pad_add_fusion.where_ref, bf16[128,256]{1,0:T(8,128)(2,1)S(1)} %collective-permute-done.1.low_ref, bf16[128,256]{1,0:T(8,128)(2,1)S(1)} %reduce_sum.9.mid_ref, bf16[128,256]{1,0:T(8,128)(2,1)S(1)} %collective-permute-done.2.high_ref, ...), custom_call_target="tpu_custom_call" | custom-call | flops 4697620480 | bytes 1048576 | tf_op jit(solution)/shard_map/pallas_call | solution.py:106
  59.6 3.7 %all-gather.1 = bf16[512,512]{1,0:T(8,128)(2,1)S(1)} all-gather(bf16[256,512]{1,0:T(8,128)(2,1)S(1)} %shard_map.120), channel_id=3, replica_groups=mesh['band'=128,'ch'=2] {'ch'}, dimensions={0}, use_global_device_ids=true | all-gather | bytes 786432 | tf_op jit(solution)/shard_map/all_gather | solution.py:214
  63.4 1.1 %shard_map.121 = bf16[256,512]{1,0:T(8,128)(2,1)S(1)} custom-call(s32[2]{0:T(128)S(1)} %pad_add_fusion.where_ref, bf16[2,256,512]{2,1,0:T(8,128)(2,1)S(1)} %bitcast.30, bf16[512,512]{1,0:T(8,128)(2,1)S(1)} %convolution_convert_fusion.1.own_ref, bf16[512,512]{1,0:T(8,128)(2,1)S(1)} %convolution_convert_fusion.other_ref, ...), custom_call_target="tpu_custom_call" | custom-call | flops 268435456 | bytes 1048576 | tf_op jit(solution)/shard_map/pallas_call | solution.py:106
  64.4 2.2 %all-gather.2 = bf16[512,512]{1,0:T(8,128)(2,1)S(1)} all-gather(bf16[256,512]{1,0:T(8,128)(2,1)S(1)} %shard_map.121), channel_id=4, replica_groups=mesh['band'=128,'ch'=2] {'ch'}, dimensions={0}, use_global_device_ids=true | all-gather | bytes 786432 | tf_op jit(solution)/shard_map/all_gather | solution.py:223
  66.6 2.3 %shard_map.122 = bf16[256,512]{1,0:T(8,128)(2,1)} custom-call(s32[2]{0:T(128)S(1)} %pad_add_fusion.where_ref, bf16[2,256,512]{2,1,0:T(8,128)(2,1)S(1)} %bitcast.29, bf16[512,512]{1,0:T(8,128)(2,1)S(1)} %copy-done.3, bf16[512,512]{1,0:T(8,128)(2,1)} %collective-permute-done.4.other_ref, bf16[128,256]{1,0:T(8,128)(2,1)S(1)} %reduce_sum.9.mid_ref, ...), custom_call_target="tpu_custom_call" | custom-call | flops 268435456 | bytes 1048576 | tf_op jit(solution)/shard_map/pallas_call | solution.py:106
  (48 shorter events, 4.7 us)
Async XLA Ops:
  0.0 9.3 %copy-start.8 = (bf16[512,1024]{1,0:T(8,128)(2,1)S(1)}, bf16[512,1024]{1,0:T(8,128)(2,1)}, u32[]{:S(2)}) copy-start(bf16[512,1024]{1,0:T(8,128)(2,1)} %param.23) | copy-start | bytes 3145732
  0.8 10.4 %copy-start.11 = (bf16[100,512]{1,0:T(8,128)(2,1)S(1)}, bf16[100,512]{1,0:T(8,128)(2,1)}, u32[]{:S(2)}) copy-start(bf16[100,512]{1,0:T(8,128)(2,1)} %param.17) | copy-start | bytes 307204
  0.8 13.1 %copy-start.14 = (bf16[2,1024,512]{2,1,0:T(8,128)(2,1)S(1)}, bf16[2,1024,512]{2,1,0:T(8,128)(2,1)}, u32[]{:S(2)}) copy-start(bf16[2,1024,512]{2,1,0:T(8,128)(2,1)} %param.20) | copy-start | bytes 6291460
  3.9 28.3 %collective-permute-start = (bf16[100,8192]{1,0:T(8,128)(2,1)}, bf16[100,8192]{1,0:T(8,128)(2,1)}, u32[]{:S(2)}, u32[]{:S(2)}) collective-permute-start(bf16[100,8192]{1,0:T(8,128)(2,1)} %dynamic-slice_select_fusion), channel_id=1, source_target_pairs={{0,2},{2,4},{4,6},{6,8},{8,10},{10,12},{12,14},{14,16},{16,18},{18... | collective-permute-start | bytes 4915208 | tf_op jit(solution)/shard_map/ppermute | solution.py:146
  6.4 37.9 %collective-permute-start.3 = (bf16[512,1024]{1,0:T(8,128)(2,1)}, bf16[512,1024]{1,0:T(8,128)(2,1)}, u32[]{:S(2)}, u32[]{:S(2)}) collective-permute-start(bf16[512,1024]{1,0:T(8,128)(2,1)} %param.21), channel_id=1, source_target_pairs={{0,1},{1,0},{2,3},{3,2},{4,5},{5,4},{6,7},{7,6},{8,9},{9,8},{10,11... | collective-permute-start | bytes 3145736 | tf_op jit(solution)/shard_map/ppermute | solution.py:150
  10.4 56.2 %collective-permute-start.4 = (bf16[512,512]{1,0:T(8,128)(2,1)}, bf16[512,512]{1,0:T(8,128)(2,1)}, u32[]{:S(2)}, u32[]{:S(2)}) collective-permute-start(bf16[512,512]{1,0:T(8,128)(2,1)} %get-tuple-element.5), channel_id=1, source_target_pairs={{0,1},{1,0},{2,3},{3,2},{4,5},{5,4},{6,7},{7,6},{8,9},{9,8},{10,11... | collective-permute-start | bytes 1572872 | tf_op jit(solution)/shard_map/ppermute | solution.py:153
  11.1 6.5 %copy-start.13 = (s32[5120]{0:T(1024)S(1)}, s32[5120]{0:T(1024)}, u32[]{:S(2)}) copy-start(s32[5120]{0:T(1024)} %param.18) | copy-start | bytes 61444
  13.2 0.7 copy-start.12
  14.2 8.6 %copy-start.2 = (bf16[100,16384]{1,0:T(8,128)(2,1)S(1)}, bf16[100,16384]{1,0:T(8,128)(2,1)}, u32[]{:S(2)}) copy-start(bf16[100,16384]{1,0:T(8,128)(2,1)} %points_ref.1) | copy-start | bytes 9830404
  14.2 8.6 %copy-start.7 = (s32[1,16]{1,0:T(1,128)S(1)}, s32[1,16]{1,0:T(1,128)}, u32[]{:S(2)}) copy-start(s32[1,16]{1,0:T(1,128)} %ids_ref.3) | copy-start | bytes 196
  22.9 2.2 %copy-start = (bf16[1,16,256,512]{3,2,1,0:T(8,128)(2,1)S(1)}, bf16[1,16,256,512]{3,2,1,0:T(8,128)(2,1)}, u32[]{:S(2)}) copy-start(bf16[1,16,256,512]{3,2,1,0:T(8,128)(2,1)} %param.16) | copy-start | bytes 12582916
  25.1 1.2 %copy-start.9 = (bf16[512,100]{1,0:T(8,128)(2,1)S(1)}, bf16[512,100]{1,0:T(8,128)(2,1)}, u32[]{:S(2)}) copy-start(bf16[512,100]{1,0:T(8,128)(2,1)} %copy.15) | copy-start | bytes 307204
  25.1 1.2 %copy-start.10 = (bf16[512,100]{1,0:T(8,128)(2,1)S(1)}, bf16[512,100]{1,0:T(8,128)(2,1)}, u32[]{:S(2)}) copy-start(bf16[512,100]{1,0:T(8,128)(2,1)} %copy.16) | copy-start | bytes 307204
  25.1 1.7 %copy-start.15 = (bf16[2,1024,512]{2,1,0:T(8,128)(2,1)S(1)}, bf16[2,1024,512]{2,1,0:T(8,128)(2,1)}, u32[]{:S(2)}) copy-start(bf16[2,1024,512]{2,1,0:T(8,128)(2,1)} %param.22) | copy-start | bytes 6291460
  25.1 2.0 %copy-start.17 = (bf16[512,1024]{1,0:T(8,128)(2,1)S(1)}, bf16[512,1024]{1,0:T(8,128)(2,1)}, u32[]{:S(2)}) copy-start(bf16[512,1024]{1,0:T(8,128)(2,1)} %param.21) | copy-start | bytes 3145732
  25.1 7.2 %copy-start.1 = (bf16[1,16,256,512]{3,2,1,0:T(8,128)(2,1)S(1)}, bf16[1,16,256,512]{3,2,1,0:T(8,128)(2,1)}, u32[]{:S(2)}) copy-start(bf16[1,16,256,512]{3,2,1,0:T(8,128)(2,1)} %param.16) | copy-start | bytes 12582916
  27.8 16.6 %copy-start.16 = (bf16[2,1024,512]{2,1,0:T(8,128)(2,1)S(1)}, bf16[2,1024,512]{2,1,0:T(8,128)(2,1)}, u32[]{:S(2)}) copy-start(bf16[2,1024,512]{2,1,0:T(8,128)(2,1)} %param.22) | copy-start | bytes 6291460
  34.3 18.5 %copy-start.5 = (s32[5,1024]{1,0:T(8,128)S(1)}, s32[5,1024]{1,0:T(8,128)}, u32[]{:S(2)}) copy-start(s32[5,1024]{1,0:T(8,128)} %reshape.13.src_ref) | copy-start | bytes 61444
  34.3 18.5 %copy-start.6 = (s32[5,1024]{1,0:T(8,128)S(1)}, s32[5,1024]{1,0:T(8,128)}, u32[]{:S(2)}) copy-start(s32[5,1024]{1,0:T(8,128)} %reshape.14.dst_ref) | copy-start | bytes 61444
  36.4 9.9 %collective-permute-start.1 = (bf16[128,256]{1,0:T(8,128)(2,1)S(1)}, bf16[128,256]{1,0:T(8,128)(2,1)S(1)}, u32[]{:S(2)}, u32[]{:S(2)}) collective-permute-start(bf16[128,256]{1,0:T(8,128)(2,1)S(1)} %reduce_sum.9.mid_ref), channel_id=1, source_target_pairs={{0,2},{2,4},{4,6},{6,8},{8,10},{10,12},{12,14},{14,16},{16,18},{18... | collective-permute-start | bytes 196616 | tf_op jit(solution)/shard_map/ppermute | solution.py:192
  42.4 10.4 %collective-permute-start.2 = (bf16[128,256]{1,0:T(8,128)(2,1)S(1)}, bf16[128,256]{1,0:T(8,128)(2,1)S(1)}, u32[]{:S(2)}, u32[]{:S(2)}) collective-permute-start(bf16[128,256]{1,0:T(8,128)(2,1)S(1)} %reduce_sum.9.mid_ref), channel_id=1, source_target_pairs={{2,0},{4,2},{6,4},{8,6},{10,8},{12,10},{14,12},{16,14},{18,16},{20... | collective-permute-start | bytes 196616 | tf_op jit(solution)/shard_map/ppermute | solution.py:193
  46.3 17.1 %copy-start.4 = (bf16[128,512]{1,0:T(8,128)(2,1)S(1)}, bf16[128,512]{1,0:T(8,128)(2,1)}, u32[]{:S(2)}) copy-start(bf16[128,512]{1,0:T(8,128)(2,1)} %pad.16.direct_ref) | copy-start | bytes 393220
  59.6 7.0 %copy-start.3 = (bf16[512,512]{1,0:T(8,128)(2,1)S(1)}, bf16[512,512]{1,0:T(8,128)(2,1)}, u32[]{:S(2)}) copy-start(bf16[512,512]{1,0:T(8,128)(2,1)} %get-tuple-element.6.own_ref) | copy-start | bytes 1572868

commit v2 on v1

v2 whole, which is shorter than its diff:
```python
import jax
import jax.numpy as jnp
from jax import lax
from jax.experimental import pallas as pl
from jax.experimental.pallas import tpu as pltpu
from jax.sharding import PartitionSpec as P

F32 = jnp.float32
BF16 = jnp.bfloat16
VMEM = pl.BlockSpec(memory_space=pltpu.VMEM)
HBM = pl.BlockSpec(memory_space=pltpu.HBM)
SMEM = pl.BlockSpec(memory_space=pltpu.SMEM)
NT = (((1,), (1,)), ((), ()))
TN = (((0,), (0,)), ((), ()))


def silu(v):
    return v * (0.5 * jnp.tanh(0.5 * v) + 0.5)


def pack_kernel(band_points_ref, points_ref, out_ref, limit_ref, limit_sem, sems):
    core = lax.axis_index("ch")
    half = out_ref.shape[1]
    parts = sems.shape[0]
    width = half // parts
    limit_copy = pltpu.make_async_copy(band_points_ref, limit_ref, limit_sem)
    limit_copy.start()
    copies = []
    for i in range(parts):
        start = pl.multiple_of((1 - core) * half + i * width, width)
        copies.append(
            pltpu.make_async_copy(
                points_ref.at[:, pl.ds(start, width)],
                out_ref.at[:, i * width : (i + 1) * width],
                sems.at[i],
            )
        )
        copies[-1].start()
    limit_copy.wait()
    for i in range(parts):
        copies[i].wait()

        @pl.when((core == 0) & (half + (i + 1) * width > limit_ref[0]))
        def _():
            x = out_ref[:, i * width : (i + 1) * width]
            column = half + i * width + lax.broadcasted_iota(jnp.int32, x.shape, 1)
            out_ref[:, i * width : (i + 1) * width] = jnp.where(
                column < limit_ref[0], x, jnp.zeros_like(x)
            )


def own_kernel(
    ids_ref, count_ref, limit_ref, weight_ref, points_ref, out_ref,
):
    band, core = lax.axis_index("band"), lax.axis_index("ch")
    channels = points_ref.shape[0]
    kblocks, _, block_len = weight_ref.shape
    sub_count = points_ref.shape[1] // block_len
    out_ref[...] = jnp.zeros_like(out_ref)
    for k in range(kblocks):
        local = ids_ref[0, k] - band * sub_count
        mine = (local >= 0) & (local < sub_count) & (core == k % 2) & (k < count_ref[0])

        @pl.when(mine)
        def _():
            at = pl.multiple_of(local * block_len, block_len)
            x = points_ref[:, pl.ds(at, block_len)]
            column = at + lax.broadcasted_iota(jnp.int32, x.shape, 1)
            x = jnp.where(column < limit_ref[0], x, jnp.zeros_like(x))
            out_ref[:channels, :] += lax.dot_general(
                x, weight_ref[k], NT, preferred_element_type=F32
            )


def halo_kernel(ids_ref, count_ref, weight_ref, points_ref, own_ref, out_ref, slots):
    band, core = lax.axis_index("band"), lax.axis_index("ch")
    channels = points_ref.shape[0]
    kblocks, _, block_len = weight_ref.shape
    blocks = points_ref.shape[1] // block_len
    sub_count = 2 * blocks
    found = jnp.int32(0)
    for k in range(kblocks):
        local = ids_ref[0, k] - band * sub_count
        low = (core == 0) & (local < 0)
        high = (core == 1) & (local >= sub_count)
        mine = (low | high) & (k < count_ref[0])
        block = jnp.where(low, local + blocks, local - sub_count)

        @pl.when(mine)
        def _():
            slots[0, found] = k
            slots[1, found] = jnp.clip(block, 0, blocks - 1)

        found = found + mine.astype(jnp.int32)
    out_ref[...] = own_ref[...]
    group = 4
    for first in range(0, kblocks, group):

        @pl.when(first < found)
        def _():
            total = None
            for j in range(first, first + group):
                used = j < found
                k = jnp.where(used, slots[0, j], 0)
                block = jnp.where(used, slots[1, j], 0)
                at = pl.multiple_of(block * block_len, block_len)
                x = points_ref[:, pl.ds(at, block_len)]
                x = jnp.where(used, x, jnp.zeros_like(x))
                part = lax.dot_general(x, weight_ref[k], NT, preferred_element_type=F32)
                total = part if total is None else total + part
            out_ref[:channels, :] += total


def weights_kernel(
    embed_ref, embed_other_ref, edge_in_ref, node_own_ref, node_other_ref,
    out_own_ref, out_other_ref, into_ref, direct_ref, agg_ref,
):
    core = lax.axis_index("ch")
    channels, share = embed_ref.shape
    own = pl.ds(pl.multiple_of(core * share, share), share)
    other = pl.ds(pl.multiple_of((1 - core) * share, share), share)

    def dot(a, b):
        return jnp.dot(a, b, preferred_element_type=F32)

    rows = direct_ref.shape[0]
    into_ref[...] = jnp.zeros_like(into_ref)
    direct_ref[...] = jnp.zeros_like(direct_ref)
    for i in range(2):
        v = dot(embed_ref[...], edge_in_ref[i, own, :])
        v += dot(embed_other_ref[...], edge_in_ref[i, other, :])
        into_ref[i * rows : i * rows + channels, :] = v.astype(BF16)
    for j, node_ref in enumerate((node_own_ref, node_other_ref)):
        columns = slice(j * share, (j + 1) * share)
        v = dot(embed_ref[...], node_ref[0, own, :])
        v += dot(embed_other_ref[...], node_ref[0, other, :])
        direct_ref[:channels, columns] = v.astype(BF16)
        for i, half_ref in enumerate((out_own_ref, out_other_ref)):
            agg_ref[i, :, columns] = dot(half_ref[...], node_ref[1]).astype(BF16)


def edge_kernel(near_ref, mid_ref, into_ref, src_ref, dst_ref, out_ref, acc_ref):
    band = lax.axis_index("band")
    rows, nodes = mid_ref.shape
    edges = src_ref.shape[1]
    size = edges // 2
    sources = jnp.concatenate([near_ref[0], mid_ref[...], near_ref[1]], axis=0)
    node = lax.broadcasted_iota(jnp.int32, (nodes, size), 0).astype(F32).astype(BF16)
    one, zero = jnp.ones((), BF16), jnp.zeros((), BF16)

    def before(at):
        src = src_ref[:, at : at + size] - (band - 1) * nodes
        dst = dst_ref[:, at : at + size] - band * nodes
        piece = src // nodes
        from_hot = jnp.where(node == (src - piece * nodes).astype(F32).astype(BF16), one, zero)
        to_hot = jnp.where(node == dst.astype(F32).astype(BF16), one, zero)
        got = jnp.dot(sources, from_hot, preferred_element_type=F32)
        a, b, c = got[:rows], got[rows : 2 * rows], got[2 * rows :]
        from_src = jnp.where(piece == 0, a, jnp.where(piece == 1, b, c))
        from_dst = jnp.dot(mid_ref[...], to_hot, preferred_element_type=F32)
        both = jnp.concatenate([from_src.astype(BF16), from_dst.astype(BF16)], axis=0)
        return lax.dot_general(into_ref[...], both, TN, preferred_element_type=F32), to_hot

    acc_ref[...] = jnp.zeros_like(acc_ref)
    now = before(0)
    for at in range(0, edges, size):
        later = before(at + size) if at + size < edges else None
        pre, to_hot = now
        hidden = silu(pre).astype(BF16)
        acc_ref[...] += lax.dot_general(to_hot, hidden, NT, preferred_element_type=F32)
        now = later
    out_ref[...] = acc_ref[...].astype(out_ref.dtype)


def node_kernel(
    sums_ref, mid_ref, direct_ref, embed_ref, agg_hbm, last_own_hbm, last_other_hbm, out_ref,
    agg_ref, last_ref, sems,
):
    core = lax.axis_index("ch")
    channels, share = embed_ref.shape
    columns = pl.ds(pl.multiple_of(core * share, share), share)
    copies = [
        pltpu.make_async_copy(agg_hbm.at[0], agg_ref.at[0], sems.at[0]),
        pltpu.make_async_copy(agg_hbm.at[1], agg_ref.at[1], sems.at[1]),
        pltpu.make_async_copy(last_own_hbm.at[:, columns], last_ref.at[0], sems.at[2]),
        pltpu.make_async_copy(last_other_hbm.at[:, columns], last_ref.at[1], sems.at[3]),
    ]
    for copy in copies:
        copy.start()
    v = lax.dot_general(mid_ref[...], direct_ref[...], TN, preferred_element_type=F32)
    copies[0].wait()
    v += jnp.dot(sums_ref[core], agg_ref[0], preferred_element_type=F32)
    copies[1].wait()
    v += jnp.dot(sums_ref[1 - core], agg_ref[1], preferred_element_type=F32)
    update = silu(v).astype(BF16)
    v = lax.dot_general(mid_ref[:channels, :], embed_ref[...], TN, preferred_element_type=F32)
    copies[2].wait()
    v += jnp.dot(update[:, :share], last_ref[0], preferred_element_type=F32)
    copies[3].wait()
    v += jnp.dot(update[:, share:], last_ref[1], preferred_element_type=F32)
    out_ref[...] = v.astype(out_ref.dtype)


def call(kernel, out, specs, limit_mib, flops, args, scratch=()):
    return pl.pallas_call(
        kernel,
        out_shape=out,
        in_specs=specs,
        out_specs=[VMEM] * len(out) if isinstance(out, tuple) else VMEM,
        scratch_shapes=list(scratch),
        compiler_params=pltpu.CompilerParams(vmem_limit_bytes=int(limit_mib * 2**20)),
        cost_estimate=pl.CostEstimate(flops=flops, bytes_accessed=1 << 20, transcendentals=0),
    )(*args)


def on_device(
    grid_field,
    band_points,
    block_ids,
    block_count,
    block_weight,
    embed_weight,
    edge_src,
    edge_dst,
    edge_in_weight,
    edge_out_weight,
    node_in_weight,
    node_out_weight,
):
    bands = lax.axis_size("band")
    channels, points = grid_field.shape
    _, kblocks, nodes, block_len = block_weight.shape
    share = embed_weight.shape[1]
    edges = edge_src.shape[0]
    half = points // 2
    rows = -(-channels // 16) * 16
    weight = block_weight[0]
    shape = jax.ShapeDtypeStruct

    pairs = [(2 * b, 2 * b + 2) for b in range(bands - 1)]
    pairs += [(2 * b + 3, 2 * b + 1) for b in range(bands - 1)]
    piece = call(
        pack_kernel,
        pltpu.VMEM((channels, half), BF16),
        [HBM, HBM],
        61,
        1 << 20,
        (band_points, grid_field),
        [pltpu.SMEM((1,), jnp.int32), pltpu.SemaphoreType.DMA, pltpu.SemaphoreType.DMA((8,))],
    )
    halo = lax.ppermute(piece, ("band", "ch"), pairs)

    def partner(x):
        return lax.ppermute(x, "ch", [(0, 1), (1, 0)])

    embed_other = partner(embed_weight)
    out_other = partner(edge_out_weight)
    node_other = partner(node_in_weight)
    last_other = partner(node_out_weight)
    src, dst = edge_src.reshape(1, edges), edge_dst.reshape(1, edges)
    remap_flops = 2 * channels * nodes * block_len * kblocks // 4
    sums = shape((rows, nodes), F32)
    partial = call(
        own_kernel,
        sums,
        [SMEM] * 3 + [VMEM] * 2,
        16,
        8 * remap_flops,
        (block_ids, block_count, band_points, weight, grid_field),
    )
    into_edge, direct, agg = call(
        weights_kernel,
        (
            shape((2 * rows, share), BF16),
            shape((rows, 2 * share), BF16),
            shape((2, share, 2 * share), BF16),
        ),
        [VMEM] * 7,
        16,
        16 * share**3,
        (
            embed_weight,
            embed_other,
            edge_in_weight,
            node_in_weight,
            node_other,
            edge_out_weight,
            out_other,
        ),
    )

    partial = call(
        halo_kernel,
        sums,
        [SMEM] * 2 + [VMEM] * 3,
        12,
        remap_flops,
        (block_ids, block_count, weight, halo, partial),
        [pltpu.SMEM((2, kblocks), jnp.int32)],
    )
    mid = lax.all_gather(partial, "ch").sum(axis=0).astype(BF16)
    near = lax.ppermute(mid, ("band", "ch"), pairs)
    near = lax.all_gather(near, "ch")
    by_node = call(
        edge_kernel,
        shape((nodes, share), BF16),
        [VMEM] * 5,
        24,
        2 * edges * nodes * 7 * 256,
        (near, mid, into_edge, src, dst),
        [pltpu.VMEM((nodes, share), F32)],
    )
    return call(
        node_kernel,
        shape((nodes, share), BF16),
        [VMEM] * 4 + [HBM] * 3,
        61,
        2 * nodes * share * 6 * share,
        (
            lax.all_gather(by_node, "ch"),
            mid,
            direct,
            embed_weight,
            agg,
            node_out_weight,
            last_other,
        ),
        [
            pltpu.VMEM((2, share, 2 * share), BF16),
            pltpu.VMEM((2, share, share), BF16),
            pltpu.SemaphoreType.DMA((4,)),
        ],
    )


def solution(mesh):
    return jax.shard_map(
        on_device,
        mesh=mesh,
        in_specs=(
            P(None, "band"),
            P("band"),
            P("band", None),
            P("band"),
            P("band", None, None, None),
            P(None, "ch"),
            P("band"),
            P("band"),
            P(None, None, "ch"),
            P("ch", None),
            P(None, None, "ch"),
            P("ch", None),
        ),
        out_specs=P("band", "ch"),
        check_vma=False,
    )
```

time: 69.4 us -> 71.4 us (1.029)
  the two profiles are of different devices: /device:TPU:127 before, /device:TPU:129 now
where the time goes in v2:
time: 71.4 us; the launch traced here: 70.9 us
  Pallas kernels  18.9 us (26%)
  blocking collectives  14.2 us (20%)
  starting transfers between devices  13.8 us (19%)
  waiting for transfers between devices  13.8 us (19%)
  local copies, waits for them, and re-layouts  7.78 us (11%)
  between operations  1.47 us (2%)
  other arithmetic  0.96 us (1%)
    pallas_call x6, Pallas kernels, call(): pl.pallas_call(kernel, out_shape=out, in_specs=specs, out_specs=[VMEM] *...  18.9 us
    ppermute x1, waiting for transfers between devices, on_device(): halo = lax.ppermute(piece, ('band', 'ch'), pairs)  12.6 us
    unnamed x24, local copies, waits for them, and re-layouts  7.78 us
    ppermute x1, starting transfers between devices, on_device(): halo = lax.ppermute(piece, ('band', 'ch'), pairs)  6.38 us
    all_gather x1, blocking collectives, on_device(): near = lax.all_gather(near, 'ch')  6.24 us
    ppermute x1, starting transfers between devices, on_device(): near = lax.ppermute(mid, ('band', 'ch'), pairs)  6.03 us
    all_gather x1, blocking collectives, on_device(): mid = lax.all_gather(partial, 'ch').sum(axis=0).astype(BF16)  5.67 us
    all_gather x1, blocking collectives, on_device(): lax.all_gather(by_node, 'ch')  2.31 us
  transfers between devices with their start and end apart: 6, of which 2 were waited for; matrix products, arithmetic and copies ran while one was open for 1% of the time, Pallas kernels for 20%

profile of v2, /device:TPU:129, one launch (start us, length us, event | category | flops | bytes accessed | tf_op | source)
XLA Modules:
  0.0 70.9 jit_solution(149895390405840321)
XLA Ops:
  0.0 0.7 collective-permute-start.3
  1.3 0.0 copy-start.6
  1.4 2.9 %shard_map.118 = bf16[100,8192]{1,0:T(8,128)(2,1)} custom-call(s32[1]{0:T(128)S(6)} %copy.13.band_points_ref.limit_ref, bf16[100,16384]{1,0:T(8,128)(2,1)} %points_ref.3), custom_call_target="tpu_custom_call" | custom-call | flops 1048576 | bytes 1048576 | tf_op jit(solution)/shard_map/pallas_call | solution.py:205
  4.2 6.4 %collective-permute-start = (bf16[100,8192]{1,0:T(8,128)(2,1)}, bf16[100,8192]{1,0:T(8,128)(2,1)S(1)}, u32[]{:S(2)}, u32[]{:S(2)}) collective-permute-start(bf16[100,8192]{1,0:T(8,128)(2,1)} %shard_map.118), channel_id=1, source_target_pairs={{0,2},{2,4},{4,6},{6,8},{8,10},{10,12},{12,14},{14,16},{16,18},{18... | collective-permute-start | bytes 4915208 | tf_op jit(solution)/shard_map/ppermute | solution.py:251
  10.6 0.1 collective-permute-start.4
  10.7 0.5 collective-permute-start.5
  11.2 0.1 collective-permute-start.2
  12.0 2.2 %copy-done = bf16[1,16,256,512]{3,2,1,0:T(8,128)(2,1)S(1)} copy-done((bf16[1,16,256,512]{3,2,1,0:T(8,128)(2,1)S(1)}, bf16[1,16,256,512]{3,2,1,0:T(8,128)(2,1)}, u32[]{:S(2)}) %copy-start) | copy-done | bytes 4194328
  14.2 2.0 %copy-done.1 = bf16[100,16384]{1,0:T(8,128)(2,1)S(1)} copy-done((bf16[100,16384]{1,0:T(8,128)(2,1)S(1)}, bf16[100,16384]{1,0:T(8,128)(2,1)}, u32[]{:S(2)}) %copy-start.1) | copy-done | bytes 3276824
  16.1 0.9 %shard_map.119.own_ref = f32[112,256]{1,0:T(8,128)S(1)} custom-call(s32[1,16]{1,0:T(1,128)S(1)} %copy-done.9, s32[1]{0:T(128)S(6)} %copy.14.count_ref, s32[1]{0:T(128)S(6)} %copy.13.band_points_ref.limit_ref, bf16[16,256,512]{2,1,0:T(8,128)(2,1)S(1)} %bitcast.6, bf16[100,16384]{1,0:T(8,128)(2,1)S(1)} %copy-done.1), custom_call_target="tpu_custom_call" | custom-call | flops 838860800 | bytes 1048576 | tf_op jit(solution)/shard_map/pallas_call | solution.py:205
  17.1 12.6 %collective-permute-done.points_ref = bf16[100,8192]{1,0:T(8,128)(2,1)S(1)} collective-permute-done((bf16[100,8192]{1,0:T(8,128)(2,1)}, bf16[100,8192]{1,0:T(8,128)(2,1)S(1)}, u32[]{:S(2)}, u32[]{:S(2)}) %collective-permute-start) | collective-permute-done | bytes 1638432 | tf_op jit(solution)/shard_map/ppermute | solution.py:251
  29.7 1.2 %shard_map.120 = f32[112,256]{1,0:T(8,128)S(1)} custom-call(s32[1,16]{1,0:T(1,128)S(1)} %copy-done.9, s32[1]{0:T(128)S(6)} %copy.14.count_ref, bf16[16,256,512]{2,1,0:T(8,128)(2,1)S(1)} %bitcast.7, bf16[100,8192]{1,0:T(8,128)(2,1)S(1)} %collective-permute-done.points_ref, f32[112,256]{1,0:T(8,128)S(1)} %shard_map.119.own_ref), custom_call_target="tpu_custom_call" | custom-call | flops 104857600 | bytes 1048576 | tf_op jit(solution)/shard_map/pallas_call | solution.py:205
  30.8 5.7 %all-gather = f32[224,256]{1,0:T(8,128)} all-gather(f32[112,256]{1,0:T(8,128)S(1)} %shard_map.120), channel_id=2, replica_groups=mesh['band'=128,'ch'=2] {'ch'}, dimensions={0}, use_global_device_ids=true | all-gather | bytes 344064 | tf_op jit(solution)/shard_map/all_gather | solution.py:301
  36.5 1.0 %reduce_sum.9.mid_ref = bf16[112,256]{1,0:T(8,128)(2,1)S(1)} reduce(f32[2,112,256]{2,1,0:T(8,128)} %bitcast.12, f32[]{:T(128)} %constant.0.clone.1), dimensions={0}, to_apply=%region_0.0 | reduce | flops 28672 | bytes 286724 | tf_op jit(solution)/shard_map/reduce_sum | solution.py:301
  37.5 6.0 %collective-permute-start.1 = (bf16[112,256]{1,0:T(8,128)(2,1)S(1)}, bf16[112,256]{1,0:T(8,128)(2,1)S(1)}, u32[]{:S(2)}, u32[]{:S(2)}) collective-permute-start(bf16[112,256]{1,0:T(8,128)(2,1)S(1)} %reduce_sum.9.mid_ref), channel_id=1, source_target_pairs={{0,2},{2,4},{4,6},{6,8},{8,10},{10,12},{12,14},{14,16},{16,18},{18... | collective-permute-start | bytes 172040 | tf_op jit(solution)/shard_map/ppermute | solution.py:302
  43.5 1.2 %collective-permute-done.1 = bf16[112,256]{1,0:T(8,128)(2,1)S(1)} collective-permute-done((bf16[112,256]{1,0:T(8,128)(2,1)S(1)}, bf16[112,256]{1,0:T(8,128)(2,1)S(1)}, u32[]{:S(2)}, u32[]{:S(2)}) %collective-permute-start.1) | collective-permute-done | bytes 57376 | tf_op jit(solution)/shard_map/ppermute | solution.py:302
  44.8 6.2 %all-gather.1 = bf16[224,256]{1,0:T(8,128)(2,1)S(1)} all-gather(bf16[112,256]{1,0:T(8,128)(2,1)S(1)} %collective-permute-done.1), channel_id=3, replica_groups=mesh['band'=128,'ch'=2] {'ch'}, dimensions={0}, use_global_device_ids=true | all-gather | bytes 172032 | tf_op jit(solution)/shard_map/all_gather | solution.py:303
  51.0 1.6 %copy-done.3 = bf16[2,1024,512]{2,1,0:T(8,128)(2,1)S(1)} copy-done((bf16[2,1024,512]{2,1,0:T(8,128)(2,1)S(1)}, bf16[2,1024,512]{2,1,0:T(8,128)(2,1)}, u32[]{:S(2)}) %copy-start.3) | copy-done | bytes 2097176
  52.6 4.8 %shard_map.121 = (bf16[224,512]{1,0:T(8,128)(2,1)S(1)}, bf16[112,1024]{1,0:T(8,128)(2,1)S(1)}, bf16[2,512,1024]{2,1,0:T(8,128)(2,1)S(1)}) custom-call(bf16[100,512]{1,0:T(8,128)(2,1)S(1)} %copy-done.6, bf16[100,512]{1,0:T(8,128)(2,1)S(1)} %collective-permute-done.2.embed_other_ref, bf16[2,1024,512]{2,1,0:T(8,128)(2,1)S(1)} %copy-done.2, ...), custom_call_target="tpu_custom_call" | custom-call | flops 2147483648 | bytes 1048576 | tf_op jit(solution)/shard_map/pallas_call | solution.py:205
  57.4 1.3 %copy-done.4 = bf16[2,512,1024]{2,1,0:T(8,128)(2,1)} copy-done((bf16[2,512,1024]{2,1,0:T(8,128)(2,1)}, bf16[2,512,1024]{2,1,0:T(8,128)(2,1)S(1)}, u32[]{:S(2)}) %copy-start.4) | copy-done | bytes 2097176
  58.7 0.7 copy-done.8
  59.4 4.6 %shard_map.122 = bf16[256,512]{1,0:T(8,128)(2,1)S(1)} custom-call(bf16[2,112,256]{2,1,0:T(8,128)(2,1)S(1)} %bitcast.8, bf16[112,256]{1,0:T(8,128)(2,1)S(1)} %reduce_sum.9.mid_ref, bf16[224,512]{1,0:T(8,128)(2,1)S(1)} %get-tuple-element.8.into_ref, s32[1,5120]{1,0:T(1,128)S(1)} %bitcast.9, s32[1,5120]{1,0:T(1,128)S(1)} %bitcast.10), custom_call_target="tpu_custom_call" | custom-call | flops 4697620480 | bytes 1048576 | tf_op jit(solution)/shard_map/pallas_call | solution.py:205
  64.0 2.3 %all-gather.2 = bf16[512,512]{1,0:T(8,128)(2,1)} all-gather(bf16[256,512]{1,0:T(8,128)(2,1)S(1)} %shard_map.122), channel_id=4, replica_groups=mesh['band'=128,'ch'=2] {'ch'}, dimensions={0}, use_global_device_ids=true | all-gather | bytes 786432 | tf_op jit(solution)/shard_map/all_gather | solution.py:320
  66.3 4.6 %shard_map.123 = bf16[256,512]{1,0:T(8,128)(2,1)} custom-call(bf16[2,256,512]{2,1,0:T(8,128)(2,1)} %bitcast.11, bf16[112,256]{1,0:T(8,128)(2,1)} %copy-done.7, bf16[112,1024]{1,0:T(8,128)(2,1)} %copy-done.8, bf16[100,512]{1,0:T(8,128)(2,1)} %embed_ref.3, bf16[2,512,1024]{2,1,0:T(8,128)(2,1)} %copy-done.4, bf16[512,1024]{1,0:T(8,128)(2,1)} %last_own_hbm.1, ...), custom_call_target="tpu_custom_call" | custom-call | flops 805306368 | bytes 1048576 | tf_op jit(solution)/shard_map/pallas_call | solution.py:205
  (22 shorter events, 0.1 us)
Async XLA Ops:
  0.0 51.0 %collective-permute-start.3 = (bf16[2,1024,512]{2,1,0:T(8,128)(2,1)}, bf16[2,1024,512]{2,1,0:T(8,128)(2,1)}, u32[]{:S(2)}, u32[]{:S(2)}) collective-permute-start(bf16[2,1024,512]{2,1,0:T(8,128)(2,1)} %node_own_ref.1), channel_id=1, source_target_pairs={{0,1},{1,0},{2,3},{3,2},{4,5},{5,4},{6,7},{7,6},{8,9},{9,8},{10,11... | collective-permute-start | bytes 6291464 | tf_op jit(solution)/shard_map/ppermute | solution.py:254
  1.3 9.3 %copy-start.5 = (bf16[512,1024]{1,0:T(8,128)(2,1)S(1)}, bf16[512,1024]{1,0:T(8,128)(2,1)}, u32[]{:S(2)}) copy-start(bf16[512,1024]{1,0:T(8,128)(2,1)} %out_own_ref.1) | copy-start | bytes 3145732
  1.3 9.9 %copy-start.6 = (bf16[100,512]{1,0:T(8,128)(2,1)S(1)}, bf16[100,512]{1,0:T(8,128)(2,1)}, u32[]{:S(2)}) copy-start(bf16[100,512]{1,0:T(8,128)(2,1)} %embed_ref.3) | copy-start | bytes 307204
  1.4 10.6 %copy-start.9 = (s32[1,16]{1,0:T(1,128)S(1)}, s32[1,16]{1,0:T(1,128)}, u32[]{:S(2)}) copy-start(s32[1,16]{1,0:T(1,128)} %ids_ref.3) | copy-start | bytes 196
  4.2 25.4 %collective-permute-start = (bf16[100,8192]{1,0:T(8,128)(2,1)}, bf16[100,8192]{1,0:T(8,128)(2,1)S(1)}, u32[]{:S(2)}, u32[]{:S(2)}) collective-permute-start(bf16[100,8192]{1,0:T(8,128)(2,1)} %shard_map.118), channel_id=1, source_target_pairs={{0,2},{2,4},{4,6},{6,8},{8,10},{10,12},{12,14},{14,16},{16,18},{18... | collective-permute-start | bytes 4915208 | tf_op jit(solution)/shard_map/ppermute | solution.py:251
  10.6 40.4 %collective-permute-start.4 = (bf16[512,1024]{1,0:T(8,128)(2,1)S(1)}, bf16[512,1024]{1,0:T(8,128)(2,1)}, u32[]{:S(2)}, u32[]{:S(2)}) collective-permute-start(bf16[512,1024]{1,0:T(8,128)(2,1)S(1)} %copy-done.5), channel_id=1, source_target_pairs={{0,1},{1,0},{2,3},{3,2},{4,5},{5,4},{6,7},{7,6},{8,9},{9,8},{10,11... | collective-permute-start | bytes 3145736 | tf_op jit(solution)/shard_map/ppermute | solution.py:254
  10.7 55.6 %collective-permute-start.5 = (bf16[512,1024]{1,0:T(8,128)(2,1)}, bf16[512,1024]{1,0:T(8,128)(2,1)}, u32[]{:S(2)}, u32[]{:S(2)}) collective-permute-start(bf16[512,1024]{1,0:T(8,128)(2,1)} %last_own_hbm.1), channel_id=1, source_target_pairs={{0,1},{1,0},{2,3},{3,2},{4,5},{5,4},{6,7},{7,6},{8,9},{9,8},{10,11... | collective-permute-start | bytes 3145736 | tf_op jit(solution)/shard_map/ppermute | solution.py:254
  11.2 39.8 %collective-permute-start.2 = (bf16[100,512]{1,0:T(8,128)(2,1)S(1)}, bf16[100,512]{1,0:T(8,128)(2,1)S(1)}, u32[]{:S(2)}, u32[]{:S(2)}) collective-permute-start(bf16[100,512]{1,0:T(8,128)(2,1)S(1)} %copy-done.6), channel_id=1, source_target_pairs={{0,1},{1,0},{2,3},{3,2},{4,5},{5,4},{6,7},{7,6},{8,9},{9,8},{10,11... | collective-permute-start | bytes 307208 | tf_op jit(solution)/shard_map/ppermute | solution.py:254
  12.0 2.2 %copy-start = (bf16[1,16,256,512]{3,2,1,0:T(8,128)(2,1)S(1)}, bf16[1,16,256,512]{3,2,1,0:T(8,128)(2,1)}, u32[]{:S(2)}) copy-start(bf16[1,16,256,512]{3,2,1,0:T(8,128)(2,1)} %param.16) | copy-start | bytes 12582916
  14.2 2.0 %copy-start.1 = (bf16[100,16384]{1,0:T(8,128)(2,1)S(1)}, bf16[100,16384]{1,0:T(8,128)(2,1)}, u32[]{:S(2)}) copy-start(bf16[100,16384]{1,0:T(8,128)(2,1)} %points_ref.3) | copy-start | bytes 9830404
  17.1 33.9 %copy-start.2 = (bf16[2,1024,512]{2,1,0:T(8,128)(2,1)S(1)}, bf16[2,1024,512]{2,1,0:T(8,128)(2,1)}, u32[]{:S(2)}) copy-start(bf16[2,1024,512]{2,1,0:T(8,128)(2,1)} %edge_in_ref.1) | copy-start | bytes 6291460
  37.5 22.0 %copy-start.7 = (bf16[112,256]{1,0:T(8,128)(2,1)}, bf16[112,256]{1,0:T(8,128)(2,1)S(1)}, u32[]{:S(2)}) copy-start(bf16[112,256]{1,0:T(8,128)(2,1)S(1)} %reduce_sum.9.mid_ref) | copy-start | bytes 172036
  37.5 7.3 %collective-permute-start.1 = (bf16[112,256]{1,0:T(8,128)(2,1)S(1)}, bf16[112,256]{1,0:T(8,128)(2,1)S(1)}, u32[]{:S(2)}, u32[]{:S(2)}) collective-permute-start(bf16[112,256]{1,0:T(8,128)(2,1)S(1)} %reduce_sum.9.mid_ref), channel_id=1, source_target_pairs={{0,2},{2,4},{4,6},{6,8},{8,10},{10,12},{12,14},{14,16},{16,18},{18... | collective-permute-start | bytes 172040 | tf_op jit(solution)/shard_map/ppermute | solution.py:302
  44.8 14.7 %copy-start.10 = (s32[5120]{0:T(1024)S(1)}, s32[5120]{0:T(1024)}, u32[]{:S(2)}) copy-start(s32[5120]{0:T(1024)} %param.18) | copy-start | bytes 61444
  44.8 14.7 %copy-start.11 = (s32[5120]{0:T(1024)S(1)}, s32[5120]{0:T(1024)}, u32[]{:S(2)}) copy-start(s32[5120]{0:T(1024)} %param.19) | copy-start | bytes 61444
  51.0 1.6 %copy-start.3 = (bf16[2,1024,512]{2,1,0:T(8,128)(2,1)S(1)}, bf16[2,1024,512]{2,1,0:T(8,128)(2,1)}, u32[]{:S(2)}) copy-start(bf16[2,1024,512]{2,1,0:T(8,128)(2,1)} %node_own_ref.1) | copy-start | bytes 6291460
  57.4 1.3 %copy-start.4 = (bf16[2,512,1024]{2,1,0:T(8,128)(2,1)}, bf16[2,512,1024]{2,1,0:T(8,128)(2,1)S(1)}, u32[]{:S(2)}) copy-start(bf16[2,512,1024]{2,1,0:T(8,128)(2,1)S(1)} %get-tuple-element.10.agg_hbm) | copy-start | bytes 6291460
  58.7 0.7 copy-start.8
